TPU v7x, 64 devices: a 2x2x8 block of a 4x4x8 slice. The times are simulated.
64 devices in a mesh: data: 4 (over x, y), dap: 16 (over z, core).
Axes of the slice: x: 2, y: 2, z: 8, core: 2. Of those that a mesh axis runs over, the one named last changes fastest.
The devices are a block of a 4x4x8 slice.
Arguments:
- z: bfloat16 [1024, 256, 128], P(('data', 'dap')), parts along dimension 0
- res_mask: int32 [1024], P('data'), parts along dimension 0
- ln_w: bfloat16 [8, 2, 2, 128], replicated
- w_in: bfloat16 [8, 2, 128, 512], replicated
- b_g: bfloat16 [8, 2, 128], replicated
- w_b: bfloat16 [8, 2, 128, 4], replicated
- w_o: bfloat16 [8, 2, 128, 128], replicated
- b_o: bfloat16 [8, 2, 128], replicated
Outputs:
- output: bfloat16 [1024, 256, 128], P(('data', 'dap')), parts along dimension 0
There are 4 independent parts. A program takes and returns all parts, laid end to end along the dimension named above; an argument that names none is the same for every part.
All inputs are finite; a program needn't handle non-finite values.
Results may differ from a plain program's by a relative error of at most 0.02.
Values are sent between devices in bfloat16 or wider.
A program may use at most 768 MiB of HBM per device.

v0:
```python
import math
import jax
import jax.numpy as jnp
from jax import lax
from jax.sharding import PartitionSpec as P

EPS = 1e-5
NEG = -1e9
F32 = jnp.float32
BF16 = jnp.bfloat16


def _ln(x, w):
    x = x.astype(F32)
    mu = jnp.mean(x, axis=-1, keepdims=True)
    var = jnp.mean(jnp.square(x - mu), axis=-1, keepdims=True)
    y = (x - mu) * lax.rsqrt(var + EPS)
    return (y * w[0].astype(F32) + w[1].astype(F32)).astype(BF16)


def _rows(zl, bias, lw, wi, bg, wo, bo):
    r, n, c = zl.shape
    h = bias.shape[0]
    d = wo.shape[0] // h
    rb = math.gcd(r, 8)
    gate_b = bg.astype(F32).reshape(h, d)

    def block(zb):
        y = _ln(zb, lw)
        proj = jnp.dot(y.reshape(rb * n, c), wi, preferred_element_type=F32).reshape(rb, n, 4, h, d)
        q = proj[:, :, 0].astype(BF16)
        k = proj[:, :, 1].astype(BF16)
        v = proj[:, :, 2].astype(BF16)
        gate = jax.nn.sigmoid(proj[:, :, 3] + gate_b)
        s = jnp.einsum('bjhd,bkhd->bhjk', q, k, preferred_element_type=F32) * d ** -0.5 + bias
        p = jax.nn.softmax(s, axis=-1).astype(BF16)
        o = jnp.einsum('bhjk,bkhd->bjhd', p, v, preferred_element_type=F32)
        o = (gate * o).astype(BF16).reshape(rb * n, h * d)
        upd = jnp.dot(o, wo, preferred_element_type=F32) + bo.astype(F32)
        return (zb.astype(F32) + upd.reshape(rb, n, c)).astype(BF16)

    out = lax.map(block, zl.reshape(r // rb, rb, n, c))
    return out.reshape(r, n, c)


def _tri_start(zl, mask_bias, lw, wi, bg, wb, wo, bo):
    r, n, c = zl.shape
    b = jnp.dot(_ln(zl, lw).reshape(r * n, c), wb, preferred_element_type=F32).astype(BF16)
    b = lax.all_gather(b.reshape(r, n, -1), 'dap', axis=0, tiled=True)
    bias = jnp.transpose(b, (2, 0, 1)).astype(F32) + mask_bias
    return _rows(zl, bias, lw, wi, bg, wo, bo)


def solution(mesh):
    def local(zl, res_mask, ln_w, w_in, b_g, w_b, w_o, b_o):
        mask_bias = jnp.where(res_mask > 0, 0.0, NEG).astype(F32)
        ws = (ln_w, w_in, b_g, w_b, w_o, b_o)
        for l in range(ln_w.shape[0]):
            zl = _tri_start(zl, mask_bias, *(a[l, 0] for a in ws))
            zt = lax.all_to_all(zl, 'dap', 1, 0, tiled=True)
            zt = _tri_start(jnp.swapaxes(zt, 0, 1), mask_bias, *(a[l, 1] for a in ws))
            zl = lax.all_to_all(jnp.swapaxes(zt, 0, 1), 'dap', 0, 1, tiled=True)
        return zl

    rows = P(('data', 'dap'))
    return jax.shard_map(local, mesh=mesh,
                         in_specs=(rows, P('data'), P(), P(), P(), P(), P(), P()),
                         out_specs=rows, check_vma=False)
```

profile of v0, /device:TPU:21, one launch (start us, length us, event | category | flops | bytes accessed | tf_op | source)
XLA Modules:
  0.0 1483.0 jit_solution(5822156455808446881)
XLA Ops:
  40.6 35.7 %while.160 = (s32[]{:T(128)}, bf16[2,8,256,128]{3,1,0,2:T(8,128)(2,1)}, bf16[2,8,256,128]{3,2,1,0:T(8,128)(2,1)S(1)}, bf16[2,128]{1,0:T(2,128)(2,1)S(1)}, bf16[1...) while((s32[]{:T(128)}, ...), condition=%wide.region_7.8_spmd, body=%wide.region_2.7_spmd.sunk | while | flops 623381120 | bytes 44350384 | solution.py:42
  80.2 27.3 %all-to-all-done = bf16[16,256,128]{2,0,1:T(8,128)(2,1)S(1)} async-done(((bf16[16,256,128]{2,0,1:T(8,128)(2,1)}), bf16[16,256,128]{2,0,1:T(8,128)(2,1)S(1)}, u32[]{:S(2)}, u32[]{:S(2)}) %all-to-all-start) | async-done | bytes 1048608 | tf_op jit(solution)/shard_map/all_to_all | solution.py:60
  131.3 34.8 %while.161 = (s32[]{:T(128)}, bf16[2,8,256,128]{3,1,0,2:T(8,128)(2,1)}, bf16[2,8,256,128]{3,1,0,2:T(8,128)(2,1)S(1)}, bf16[2,128]{1,0:T(2,128)(2,1)S(1)}, bf16[1...) while((s32[]{:T(128)}, ...), condition=%wide.region_15.16_spmd, body=%wide.region_10.15_spmd.sunk | while | flops 623381120 | bytes 53787612 | solution.py:42
  172.0 27.7 %all-to-all-done.1 = bf16[256,16,128]{2,1,0:T(8,128)(2,1)S(1)} async-done(((bf16[256,16,128]{2,1,0:T(8,128)(2,1)}), bf16[256,16,128]{2,1,0:T(8,128)(2,1)S(1)}, u32[]{:S(2)}, u32[]{:S(2)}) %all-to-all-start.1) | async-done | bytes 1048608 | tf_op jit(solution)/shard_map/all_to_all | solution.py:62
  223.2 34.5 %while.162 = (s32[]{:T(128)}, bf16[2,8,256,128]{3,1,0,2:T(8,128)(2,1)}, bf16[2,8,256,128]{3,2,1,0:T(8,128)(2,1)S(1)}, bf16[2,128]{1,0:T(2,128)(2,1)S(1)}, bf16[1...) while((s32[]{:T(128)}, ...), condition=%wide.region_23.24_spmd, body=%wide.region_18.23_spmd.sunk | while | flops 623381120 | bytes 44350384 | solution.py:42
  263.2 27.7 %all-to-all-done.2 = bf16[16,256,128]{2,0,1:T(8,128)(2,1)S(1)} async-done(((bf16[16,256,128]{2,0,1:T(8,128)(2,1)}), bf16[16,256,128]{2,0,1:T(8,128)(2,1)S(1)}, u32[]{:S(2)}, u32[]{:S(2)}) %all-to-all-start.2) | async-done | bytes 1048608 | tf_op jit(solution)/shard_map/all_to_all | solution.py:60
  314.8 34.8 %while.163 = (s32[]{:T(128)}, bf16[2,8,256,128]{3,1,0,2:T(8,128)(2,1)}, bf16[2,8,256,128]{3,1,0,2:T(8,128)(2,1)S(1)}, bf16[2,128]{1,0:T(2,128)(2,1)S(1)}, bf16[1...) while((s32[]{:T(128)}, ...), condition=%wide.region_31.32_spmd, body=%wide.region_26.31_spmd.sunk | while | flops 623381120 | bytes 53787612 | solution.py:42
  355.2 27.7 %all-to-all-done.3 = bf16[256,16,128]{2,1,0:T(8,128)(2,1)S(1)} async-done(((bf16[256,16,128]{2,1,0:T(8,128)(2,1)}), bf16[256,16,128]{2,1,0:T(8,128)(2,1)S(1)}, u32[]{:S(2)}, u32[]{:S(2)}) %all-to-all-start.3) | async-done | bytes 1048608 | tf_op jit(solution)/shard_map/all_to_all | solution.py:62
  406.2 34.5 %while.164 = (s32[]{:T(128)}, bf16[2,8,256,128]{3,1,0,2:T(8,128)(2,1)}, bf16[2,8,256,128]{3,2,1,0:T(8,128)(2,1)S(1)}, bf16[2,128]{1,0:T(2,128)(2,1)S(1)}, bf16[1...) while((s32[]{:T(128)}, ...), condition=%wide.region_39.40_spmd, body=%wide.region_34.39_spmd.sunk | while | flops 623381120 | bytes 44350384 | solution.py:42
  446.3 27.7 %all-to-all-done.4 = bf16[16,256,128]{2,0,1:T(8,128)(2,1)S(1)} async-done(((bf16[16,256,128]{2,0,1:T(8,128)(2,1)}), bf16[16,256,128]{2,0,1:T(8,128)(2,1)S(1)}, u32[]{:S(2)}, u32[]{:S(2)}) %all-to-all-start.4) | async-done | bytes 1048608 | tf_op jit(solution)/shard_map/all_to_all | solution.py:60
  498.1 34.8 %while.165 = (s32[]{:T(128)}, bf16[2,8,256,128]{3,1,0,2:T(8,128)(2,1)}, bf16[2,8,256,128]{3,1,0,2:T(8,128)(2,1)S(1)}, bf16[2,128]{1,0:T(2,128)(2,1)S(1)}, bf16[1...) while((s32[]{:T(128)}, ...), condition=%wide.region_47.48_spmd, body=%wide.region_42.47_spmd.sunk | while | flops 623381120 | bytes 53787612 | solution.py:42
  539.2 27.1 %all-to-all-done.5 = bf16[256,16,128]{2,1,0:T(8,128)(2,1)S(1)} async-done(((bf16[256,16,128]{2,1,0:T(8,128)(2,1)}), bf16[256,16,128]{2,1,0:T(8,128)(2,1)S(1)}, u32[]{:S(2)}, u32[]{:S(2)}) %all-to-all-start.5) | async-done | bytes 1048608 | tf_op jit(solution)/shard_map/all_to_all | solution.py:62
  589.4 34.5 %while.166 = (s32[]{:T(128)}, bf16[2,8,256,128]{3,1,0,2:T(8,128)(2,1)}, bf16[2,8,256,128]{3,2,1,0:T(8,128)(2,1)S(1)}, bf16[2,128]{1,0:T(2,128)(2,1)S(1)}, bf16[1...) while((s32[]{:T(128)}, ...), condition=%wide.region_55.56_spmd, body=%wide.region_50.55_spmd.sunk | while | flops 623381120 | bytes 44350384 | solution.py:42
  629.5 27.7 %all-to-all-done.6 = bf16[16,256,128]{2,0,1:T(8,128)(2,1)S(1)} async-done(((bf16[16,256,128]{2,0,1:T(8,128)(2,1)}), bf16[16,256,128]{2,0,1:T(8,128)(2,1)S(1)}, u32[]{:S(2)}, u32[]{:S(2)}) %all-to-all-start.6) | async-done | bytes 1048608 | tf_op jit(solution)/shard_map/all_to_all | solution.py:60
  681.1 34.8 %while.167 = (s32[]{:T(128)}, bf16[2,8,256,128]{3,1,0,2:T(8,128)(2,1)}, bf16[2,8,256,128]{3,1,0,2:T(8,128)(2,1)S(1)}, bf16[2,128]{1,0:T(2,128)(2,1)S(1)}, bf16[1...) while((s32[]{:T(128)}, ...), condition=%wide.region_63.64_spmd, body=%wide.region_58.63_spmd.sunk | while | flops 623381120 | bytes 53787612 | solution.py:42
  721.5 27.7 %all-to-all-done.7 = bf16[256,16,128]{2,1,0:T(8,128)(2,1)S(1)} async-done(((bf16[256,16,128]{2,1,0:T(8,128)(2,1)}), bf16[256,16,128]{2,1,0:T(8,128)(2,1)S(1)}, u32[]{:S(2)}, u32[]{:S(2)}) %all-to-all-start.7) | async-done | bytes 1048608 | tf_op jit(solution)/shard_map/all_to_all | solution.py:62
  772.7 34.5 %while.168 = (s32[]{:T(128)}, bf16[2,8,256,128]{3,1,0,2:T(8,128)(2,1)}, bf16[2,8,256,128]{3,2,1,0:T(8,128)(2,1)S(1)}, bf16[2,128]{1,0:T(2,128)(2,1)S(1)}, bf16[1...) while((s32[]{:T(128)}, ...), condition=%wide.region_71.72_spmd, body=%wide.region_66.71_spmd.sunk | while | flops 623381120 | bytes 44350384 | solution.py:42
  812.7 27.7 %all-to-all-done.8 = bf16[16,256,128]{2,0,1:T(8,128)(2,1)S(1)} async-done(((bf16[16,256,128]{2,0,1:T(8,128)(2,1)}), bf16[16,256,128]{2,0,1:T(8,128)(2,1)S(1)}, u32[]{:S(2)}, u32[]{:S(2)}) %all-to-all-start.8) | async-done | bytes 1048608 | tf_op jit(solution)/shard_map/all_to_all | solution.py:60
  864.3 34.8 %while.169 = (s32[]{:T(128)}, bf16[2,8,256,128]{3,1,0,2:T(8,128)(2,1)}, bf16[2,8,256,128]{3,1,0,2:T(8,128)(2,1)S(1)}, bf16[2,128]{1,0:T(2,128)(2,1)S(1)}, bf16[1...) while((s32[]{:T(128)}, ...), condition=%wide.region_79.80_spmd, body=%wide.region_74.79_spmd.sunk | while | flops 623381120 | bytes 53787612 | solution.py:42
  904.8 27.7 %all-to-all-done.9 = bf16[256,16,128]{2,1,0:T(8,128)(2,1)S(1)} async-done(((bf16[256,16,128]{2,1,0:T(8,128)(2,1)}), bf16[256,16,128]{2,1,0:T(8,128)(2,1)S(1)}, u32[]{:S(2)}, u32[]{:S(2)}) %all-to-all-start.9) | async-done | bytes 1048608 | tf_op jit(solution)/shard_map/all_to_all | solution.py:62
  955.7 34.5 %while.170 = (s32[]{:T(128)}, bf16[2,8,256,128]{3,1,0,2:T(8,128)(2,1)}, bf16[2,8,256,128]{3,2,1,0:T(8,128)(2,1)S(1)}, bf16[2,128]{1,0:T(2,128)(2,1)S(1)}, bf16[1...) while((s32[]{:T(128)}, ...), condition=%wide.region_87.88_spmd, body=%wide.region_82.87_spmd.sunk | while | flops 623381120 | bytes 44350384 | solution.py:42
  995.8 27.7 %all-to-all-done.10 = bf16[16,256,128]{2,0,1:T(8,128)(2,1)S(1)} async-done(((bf16[16,256,128]{2,0,1:T(8,128)(2,1)}), bf16[16,256,128]{2,0,1:T(8,128)(2,1)S(1)}, u32[]{:S(2)}, u32[]{:S(2)}) %all-to-all-start.10) | async-done | bytes 1048608 | tf_op jit(solution)/shard_map/all_to_all | solution.py:60
  1047.6 34.8 %while.171 = (s32[]{:T(128)}, bf16[2,8,256,128]{3,1,0,2:T(8,128)(2,1)}, bf16[2,8,256,128]{3,1,0,2:T(8,128)(2,1)S(1)}, bf16[2,128]{1,0:T(2,128)(2,1)S(1)}, bf16[1...) while((s32[]{:T(128)}, ...), condition=%wide.region_95.96_spmd, body=%wide.region_90.95_spmd.sunk | while | flops 623381120 | bytes 53787612 | solution.py:42
  1088.0 27.7 %all-to-all-done.11 = bf16[256,16,128]{2,1,0:T(8,128)(2,1)S(1)} async-done(((bf16[256,16,128]{2,1,0:T(8,128)(2,1)}), bf16[256,16,128]{2,1,0:T(8,128)(2,1)S(1)}, u32[]{:S(2)}, u32[]{:S(2)}) %all-to-all-start.11) | async-done | bytes 1048608 | tf_op jit(solution)/shard_map/all_to_all | solution.py:62
  1139.0 34.5 %while.172 = (s32[]{:T(128)}, bf16[2,8,256,128]{3,1,0,2:T(8,128)(2,1)}, bf16[2,8,256,128]{3,2,1,0:T(8,128)(2,1)S(1)}, bf16[2,128]{1,0:T(2,128)(2,1)S(1)}, bf16[1...) while((s32[]{:T(128)}, ...), condition=%wide.region_103.104_spmd, body=%wide.region_98.103_spmd.sunk | while | flops 623381120 | bytes 44350384 | solution.py:42
  1179.0 27.7 %all-to-all-done.12 = bf16[16,256,128]{2,0,1:T(8,128)(2,1)S(1)} async-done(((bf16[16,256,128]{2,0,1:T(8,128)(2,1)}), bf16[16,256,128]{2,0,1:T(8,128)(2,1)S(1)}, u32[]{:S(2)}, u32[]{:S(2)}) %all-to-all-start.12) | async-done | bytes 1048608 | tf_op jit(solution)/shard_map/all_to_all | solution.py:60
  1230.7 34.8 %while.173 = (s32[]{:T(128)}, bf16[2,8,256,128]{3,1,0,2:T(8,128)(2,1)}, bf16[2,8,256,128]{3,1,0,2:T(8,128)(2,1)S(1)}, bf16[2,128]{1,0:T(2,128)(2,1)S(1)}, bf16[1...) while((s32[]{:T(128)}, ...), condition=%wide.region_111.112_spmd, body=%wide.region_106.111_spmd.sunk | while | flops 623381120 | bytes 53787612 | solution.py:42
  1271.1 27.7 %all-to-all-done.13 = bf16[256,16,128]{2,1,0:T(8,128)(2,1)S(1)} async-done(((bf16[256,16,128]{2,1,0:T(8,128)(2,1)}), bf16[256,16,128]{2,1,0:T(8,128)(2,1)S(1)}, u32[]{:S(2)}, u32[]{:S(2)}) %all-to-all-start.13) | async-done | bytes 1048608 | tf_op jit(solution)/shard_map/all_to_all | solution.py:62
  1322.1 34.5 %while.174 = (s32[]{:T(128)}, bf16[2,8,256,128]{3,1,0,2:T(8,128)(2,1)}, bf16[2,8,256,128]{3,2,1,0:T(8,128)(2,1)S(1)}, bf16[2,128]{1,0:T(2,128)(2,1)S(1)}, bf16[1...) while((s32[]{:T(128)}, ...), condition=%wide.region_119.120_spmd, body=%wide.region_114.119_spmd.sunk | while | flops 623381120 | bytes 44350384 | solution.py:42
  1362.2 27.7 %all-to-all-done.14 = bf16[16,256,128]{2,0,1:T(8,128)(2,1)S(1)} async-done(((bf16[16,256,128]{2,0,1:T(8,128)(2,1)}), bf16[16,256,128]{2,0,1:T(8,128)(2,1)S(1)}, u32[]{:S(2)}, u32[]{:S(2)}) %all-to-all-start.14) | async-done | bytes 1048608 | tf_op jit(solution)/shard_map/all_to_all | solution.py:60
  1413.9 34.8 %while.175 = (s32[]{:T(128)}, bf16[2,8,256,128]{3,1,0,2:T(8,128)(2,1)}, bf16[2,8,256,128]{3,1,0,2:T(8,128)(2,1)S(1)}, bf16[2,128]{1,0:T(2,128)(2,1)S(1)}, bf16[1...) while((s32[]{:T(128)}, ...), condition=%wide.region_127.128_spmd, body=%wide.region_122.127_spmd.sunk | while | flops 623381120 | bytes 53787612 | solution.py:42
  1448.7 32.5 %all_to_all.267 = bf16[256,16,128]{2,1,0:T(8,128)(2,1)S(1)} all-to-all(bf16[256,16,128]{2,1,0:T(8,128)(2,1)} %bitcast.2461), channel_id=1, replica_groups=mesh['data'=4,'dap'=16] {'dap'}, dimensions={0} | all-to-all | bytes 2097152 | tf_op jit(solution)/shard_map/all_to_all | solution.py:62
  (1152 shorter events, 1029.6 us)
Async XLA Ops:
  0.0 6.9 copy-start
  6.9 25.8 %copy-start.134 = (s32[256]{0:T(256)S(1)}, s32[256]{0:T(256)}, u32[]{:S(2)}) copy-start(s32[256]{0:T(256)} %param.41) | copy-start | bytes 3076
  76.3 31.2 %all-to-all-start = ((bf16[16,256,128]{2,0,1:T(8,128)(2,1)}), bf16[16,256,128]{2,0,1:T(8,128)(2,1)S(1)}, u32[]{:S(2)}, u32[]{:S(2)}) async-start(bf16[16,256,128]{2,0,1:T(8,128)(2,1)} %bitcast.2462), calls=%async_computation | async-start | bytes 2097152 | tf_op jit(solution)/shard_map/all_to_all | solution.py:60
  166.1 5.8 copy-start.76
  166.1 33.6 %all-to-all-start.1 = ((bf16[256,16,128]{2,1,0:T(8,128)(2,1)}), bf16[256,16,128]{2,1,0:T(8,128)(2,1)S(1)}, u32[]{:S(2)}, u32[]{:S(2)}) async-start(bf16[256,16,128]{2,1,0:T(8,128)(2,1)} %bitcast.2463), calls=%async_computation.1 | async-start | bytes 2097152 | tf_op jit(solution)/shard_map/all_to_all | solution.py:62
  257.6 5.5 copy-start.75
  257.6 33.3 %all-to-all-start.2 = ((bf16[16,256,128]{2,0,1:T(8,128)(2,1)}), bf16[16,256,128]{2,0,1:T(8,128)(2,1)S(1)}, u32[]{:S(2)}, u32[]{:S(2)}) async-start(bf16[16,256,128]{2,0,1:T(8,128)(2,1)} %bitcast.2464), calls=%async_computation.2 | async-start | bytes 2097152 | tf_op jit(solution)/shard_map/all_to_all | solution.py:60
  349.7 5.5 copy-start.74
  349.7 33.3 %all-to-all-start.3 = ((bf16[256,16,128]{2,1,0:T(8,128)(2,1)}), bf16[256,16,128]{2,1,0:T(8,128)(2,1)S(1)}, u32[]{:S(2)}, u32[]{:S(2)}) async-start(bf16[256,16,128]{2,1,0:T(8,128)(2,1)} %bitcast.2465), calls=%async_computation.3 | async-start | bytes 2097152 | tf_op jit(solution)/shard_map/all_to_all | solution.py:62
  440.7 5.5 copy-start.73
  440.7 33.3 %all-to-all-start.4 = ((bf16[16,256,128]{2,0,1:T(8,128)(2,1)}), bf16[16,256,128]{2,0,1:T(8,128)(2,1)S(1)}, u32[]{:S(2)}, u32[]{:S(2)}) async-start(bf16[16,256,128]{2,0,1:T(8,128)(2,1)} %bitcast.2466), calls=%async_computation.4 | async-start | bytes 2097152 | tf_op jit(solution)/shard_map/all_to_all | solution.py:60
  532.9 5.5 copy-start.72
  532.9 5.6 copy-start.78
  533.0 33.3 %all-to-all-start.5 = ((bf16[256,16,128]{2,1,0:T(8,128)(2,1)}), bf16[256,16,128]{2,1,0:T(8,128)(2,1)S(1)}, u32[]{:S(2)}, u32[]{:S(2)}) async-start(bf16[256,16,128]{2,1,0:T(8,128)(2,1)} %bitcast.2467), calls=%async_computation.5 | async-start | bytes 2097152 | tf_op jit(solution)/shard_map/all_to_all | solution.py:62
  623.9 5.5 copy-start.71
  623.9 33.3 %all-to-all-start.6 = ((bf16[16,256,128]{2,0,1:T(8,128)(2,1)}), bf16[16,256,128]{2,0,1:T(8,128)(2,1)S(1)}, u32[]{:S(2)}, u32[]{:S(2)}) async-start(bf16[16,256,128]{2,0,1:T(8,128)(2,1)} %bitcast.2468), calls=%async_computation.6 | async-start | bytes 2097152 | tf_op jit(solution)/shard_map/all_to_all | solution.py:60
  715.9 5.5 copy-start.70
  715.9 33.3 %all-to-all-start.7 = ((bf16[256,16,128]{2,1,0:T(8,128)(2,1)}), bf16[256,16,128]{2,1,0:T(8,128)(2,1)S(1)}, u32[]{:S(2)}, u32[]{:S(2)}) async-start(bf16[256,16,128]{2,1,0:T(8,128)(2,1)} %bitcast.2469), calls=%async_computation.7 | async-start | bytes 2097152 | tf_op jit(solution)/shard_map/all_to_all | solution.py:62
  807.1 5.5 copy-start.69
  807.1 33.3 %all-to-all-start.8 = ((bf16[16,256,128]{2,0,1:T(8,128)(2,1)}), bf16[16,256,128]{2,0,1:T(8,128)(2,1)S(1)}, u32[]{:S(2)}, u32[]{:S(2)}) async-start(bf16[16,256,128]{2,0,1:T(8,128)(2,1)} %bitcast.2470), calls=%async_computation.8 | async-start | bytes 2097152 | tf_op jit(solution)/shard_map/all_to_all | solution.py:60
  899.2 5.5 copy-start.68
  899.2 33.3 %all-to-all-start.9 = ((bf16[256,16,128]{2,1,0:T(8,128)(2,1)}), bf16[256,16,128]{2,1,0:T(8,128)(2,1)S(1)}, u32[]{:S(2)}, u32[]{:S(2)}) async-start(bf16[256,16,128]{2,1,0:T(8,128)(2,1)} %bitcast.2471), calls=%async_computation.9 | async-start | bytes 2097152 | tf_op jit(solution)/shard_map/all_to_all | solution.py:62
  990.2 5.5 copy-start.67
  990.2 33.3 %all-to-all-start.10 = ((bf16[16,256,128]{2,0,1:T(8,128)(2,1)}), bf16[16,256,128]{2,0,1:T(8,128)(2,1)S(1)}, u32[]{:S(2)}, u32[]{:S(2)}) async-start(bf16[16,256,128]{2,0,1:T(8,128)(2,1)} %bitcast.2472), calls=%async_computation.10 | async-start | bytes 2097152 | tf_op jit(solution)/shard_map/all_to_all | solution.py:60
  1082.5 5.5 copy-start.66
  1082.5 33.3 %all-to-all-start.11 = ((bf16[256,16,128]{2,1,0:T(8,128)(2,1)}), bf16[256,16,128]{2,1,0:T(8,128)(2,1)S(1)}, u32[]{:S(2)}, u32[]{:S(2)}) async-start(bf16[256,16,128]{2,1,0:T(8,128)(2,1)} %bitcast.2473), calls=%async_computation.11 | async-start | bytes 2097152 | tf_op jit(solution)/shard_map/all_to_all | solution.py:62
  1173.4 5.5 copy-start.65
  1173.4 33.3 %all-to-all-start.12 = ((bf16[16,256,128]{2,0,1:T(8,128)(2,1)}), bf16[16,256,128]{2,0,1:T(8,128)(2,1)S(1)}, u32[]{:S(2)}, u32[]{:S(2)}) async-start(bf16[16,256,128]{2,0,1:T(8,128)(2,1)} %bitcast.2474), calls=%async_computation.12 | async-start | bytes 2097152 | tf_op jit(solution)/shard_map/all_to_all | solution.py:60
  1265.5 5.5 copy-start.64
  1265.5 33.3 %all-to-all-start.13 = ((bf16[256,16,128]{2,1,0:T(8,128)(2,1)}), bf16[256,16,128]{2,1,0:T(8,128)(2,1)S(1)}, u32[]{:S(2)}, u32[]{:S(2)}) async-start(bf16[256,16,128]{2,1,0:T(8,128)(2,1)} %bitcast.2475), calls=%async_computation.13 | async-start | bytes 2097152 | tf_op jit(solution)/shard_map/all_to_all | solution.py:62
  1356.6 5.5 copy-start.63
  1356.6 33.3 %all-to-all-start.14 = ((bf16[16,256,128]{2,0,1:T(8,128)(2,1)}), bf16[16,256,128]{2,0,1:T(8,128)(2,1)S(1)}, u32[]{:S(2)}, u32[]{:S(2)}) async-start(bf16[16,256,128]{2,0,1:T(8,128)(2,1)} %bitcast.2476), calls=%async_computation.14 | async-start | bytes 2097152 | tf_op jit(solution)/shard_map/all_to_all | solution.py:60
  (180 other events, 348.2 us)
where the time goes:
time: 1490 us; the launch traced here: 1480 us
  matrix products  440 us (30%)
  waiting for transfers between devices  415 us (28%)
  blocking collectives  301 us (20%)
  local copies, waits for them, and re-layouts  145 us (10%)
  other arithmetic  95.7 us (6%)
  starting transfers between devices  80.5 us (5%)
    all_gather x16, blocking collectives, _tri_start(): b = lax.all_gather(b.reshape(r, n, -1), 'dap', axis=0, tiled=True)  268 us
    all_to_all x8, waiting for transfers between devices, local(): zt = lax.all_to_all(zl, 'dap', 1, 0, tiled=True)  221 us
    all_to_all x7, waiting for transfers between devices, local(): zl = lax.all_to_all(jnp.swapaxes(zt, 0, 1), 'dap', 0, 1, tiled=True)  194 us
    sub x32, matrix products, block(): p = jax.nn.softmax(s, axis=-1).astype(BF16)  193 us
    dot_general x32, matrix products, block(): o = jnp.einsum('bhjk,bkhd->bjhd', p, v, preferred_element_type=F32)  146 us
    dot_general x32, matrix products, block(): jnp.dot(y.reshape(rb * n, c), wi, preferred_element_type=F32)  83.9 us
    while x224, local copies, waits for them, and re-layouts  58.1 us
    reduce_sum x48, other arithmetic, _ln(): var = jnp.mean(jnp.square(x - mu), axis=-1, keepdims=True)  42.4 us
  transfers between devices with their start and end apart: 15, of which 15 were waited for; matrix products, arithmetic and copies ran while one was open for 0% of the time, Pallas kernels for 0%

commit v1 on v0

v1 whole, which is shorter than its diff:
```python
import functools
import math

import jax
import jax.numpy as jnp
from jax import lax
from jax.experimental import pallas as pl
from jax.experimental.pallas import tpu as pltpu
from jax.sharding import PartitionSpec as P

EPS = 1e-5
NEG = -1e9
LOG2E = math.log2(math.e)
F32 = jnp.float32
BF16 = jnp.bfloat16
MESH = pl.DeviceIdType.MESH
LANES = 128
ROWS = 4


def _ln(x, w):
    mu = jnp.mean(x, axis=-1, keepdims=True)
    xc = x - mu
    var = jnp.mean(xc * xc, axis=-1, keepdims=True)
    return (xc * lax.rsqrt(var + EPS) * w[0:1] + w[1:2]).astype(BF16)


def _nt(a, b):
    return lax.dot_general(a, b, (((1,), (1,)), ((), ())), preferred_element_type=F32)


def _tn(a, b):
    return lax.dot_general(a, b, (((0,), (0,)), ((), ())), preferred_element_type=F32)


def _dot(a, b):
    return jnp.dot(a, b, preferred_element_type=F32)


def _kernel(nd, nm, zin, maskb, lnw, wk, wt, bg, wb, wo, bo, out,
            zout, bout, zbuf, bbuf, zf, bf, bias, mbuf,
            zs, bs, zr, br, ms, mr):
    r, n, c = zin.shape
    passes, hd = wk.shape[0], wk.shape[2]
    heads = wb.shape[1] // 2
    d = hd // heads
    last = passes - 1
    scale = d ** -0.5 * LOG2E

    me_d, me_p = lax.axis_index("data"), lax.axis_index("dap")
    side = math.isqrt(nd)
    cube = side * side == nd and side % 2 == 0 and nm % 4 == 0
    if cube:
        sub = nm // 4
        x, y = me_d // side, me_d % side
        x0, y0 = x - x % 2, y - y % 2
        low = (x % 2) * 2 + y % 2
        mine = me_p // sub
        slot = low * sub + me_p % sub

        def home_of(crop, u):
            return (x0 + crop // 2) * side + y0 + crop % 2, u

        def cube_of(crop, u):
            lo = u // sub
            return (x0 + lo // 2) * side + y0 + lo % 2, crop * sub + u % sub
    else:
        low, mine, slot = me_d, me_d, me_p

        def home_of(crop, u):
            return me_d, u

        cube_of = home_of

    def is_me(t):
        return jnp.logical_and(t[0] == me_d, t[1] == me_p)

    def shifted(base, s):
        return (base + s) % nm

    inside = (low == mine) if cube else True

    def send(src, dst, ss, rs, target, kind, s):
        def local():
            pltpu.make_async_copy(src, dst, rs).start()

        def remote():
            pltpu.make_async_remote_copy(src, dst, ss, rs, device_id=target, device_id_type=MESH).start()

        if kind == "mid" or not cube:
            (local if s == 0 else remote)()
        else:
            me = is_me(target)
            pl.when(me)(local)
            pl.when(jnp.logical_not(me))(remote)

    def drain(ref, sem):
        pltpu.make_async_copy(ref, ref, sem).wait()

    def drain_sent(ref_all, ref_less, sem, kind):
        if kind == "mid" or not cube:
            drain(ref_less, sem)
        else:
            pl.when(inside)(lambda: drain(ref_less, sem))
            pl.when(jnp.logical_not(inside))(lambda: drain(ref_all, sem))

    barrier = pltpu.get_barrier_semaphore()
    groups = [(home_of, low), (cube_of, mine)] + ([(cube_of, low), (home_of, mine)] if cube else [])
    if not cube:
        groups = groups[:1]
    for of, crop in groups:
        def greet(u, carry, of=of, crop=crop):
            t = of(crop, u)

            @pl.when(jnp.logical_not(is_me(t)))
            def _():
                pl.semaphore_signal(barrier, inc=1, device_id=t, device_id_type=MESH)
            return carry
        lax.fori_loop(0, nm, greet, 0)
    if cube:
        @pl.when(inside)
        def _():
            pl.semaphore_wait(barrier, 4 * (nm - 1))

        @pl.when(jnp.logical_not(inside))
        def _():
            pl.semaphore_wait(barrier, 2 * (nm - 1) + 2 * nm)
    else:
        pl.semaphore_wait(barrier, nm - 1)

    low_half = lax.broadcasted_iota(jnp.int32, (2 * heads, LANES), 0) < heads

    def bias_rows(z, w, wbw):
        b = _nt(wbw, _ln(z, w))
        return jnp.where(low_half, b[:, :LANES], b[:, LANES:]).astype(BF16)

    mbuf[0] = maskb[...]
    mt = cube_of(low, me_p)
    if cube:
        me_m = is_me(mt)
        pl.when(me_m)(lambda: pltpu.make_async_copy(maskb, mbuf.at[1], mr).start())
        pl.when(jnp.logical_not(me_m))(lambda: pltpu.make_async_remote_copy(
            maskb, mbuf.at[1], ms, mr, device_id=mt, device_id_type=MESH).start())
    else:
        pltpu.make_async_copy(maskb, mbuf.at[1], mr).start()

    def first_bias(i, carry):
        w = lnw[0]
        for q in range(ROWS):
            row = i * ROWS + q
            bout[row] = bias_rows(zin[row].astype(F32), w, wb[0])
        return carry
    lax.fori_loop(0, r // ROWS, first_bias, 0)
    for s in range(nm):
        u = shifted(me_p, s)
        send(bout, bbuf.at[2, pl.ds(me_p * r, r)], bs, br.at[2], home_of(low, u), "mid", s)
    drain(bbuf.at[2], br.at[2])
    drain(bbuf.at[2, pl.ds(0, n - r)], bs)
    if cube:
        pl.when(jnp.logical_not(me_m))(lambda: drain(maskb, ms))
    drain(mbuf.at[1], mr)

    def run_pass(p, kind):
        now = 2 if kind == "first" else p % 2
        later = 2 if kind == "last" else (p + 1) % 2
        if kind != "first":
            drain(zbuf.at[now], zr.at[now])
            drain(bbuf.at[now], br.at[now])

            def widen(i, carry):
                rows = pl.ds(pl.multiple_of(i * r * r, r * r), r * r)
                zf[rows, :] = zbuf[now, pl.ds(i * r, r)].astype(F32).reshape(r * r, c)
                return carry
            lax.fori_loop(0, n // r, widen, 0)

        def widen_bias(i, carry):
            rows = pl.ds(pl.multiple_of(i * r * 2 * heads, r * 2 * heads), r * 2 * heads)
            bf[rows, :] = bbuf[now, pl.ds(i * r, r)].astype(F32).reshape(r * 2 * heads, LANES)
            return carry
        lax.fori_loop(0, n // r, widen_bias, 0)
        mask = mbuf.at[0 if kind == "first" else 1]
        for h in range(heads):
            halves = [bf[pl.ds(half * heads + h, n, stride=2 * heads), :] * LOG2E for half in range(2)]
            if kind == "first":
                halves = jnp.split(jnp.concatenate(halves, axis=1).T, 2, axis=1)
            for half in range(2):
                bias[h, :, half * LANES:(half + 1) * LANES] = halves[half] + mask[...]

        crop = low if kind == "first" else mine
        base = me_p if kind == "first" else slot
        of = home_of if kind == "last" else cube_of

        def step(i, carry):
            w = lnw[p]
            zs_, ys, ks, qvs, os = [], [], [], [], []
            for q in range(ROWS):
                row = i * ROWS + q
                if kind == "first":
                    z = zin[row].astype(F32)
                else:
                    z = zf[pl.ds(row, n, stride=r), :]
                y = _ln(z, w)
                k = _dot(y, wk[p]).astype(BF16)
                qvt = _nt(wt[p], y)
                qq = qvt[:hd].astype(BF16)
                vv = qvt[hd:2 * hd].astype(BF16)
                t = qvt[2 * hd:] + jnp.concatenate([bg[p], bg[p]], axis=1)
                g = jax.nn.sigmoid(t)
                o = []
                for h in range(heads):
                    parts = [jnp.zeros((d, n), BF16)] * heads
                    parts[h] = qq[h * d:(h + 1) * d]
                    sc = _dot(k, jnp.concatenate(parts, axis=0)) * scale + bias[h]
                    e = jnp.exp2(sc - jnp.max(sc, axis=0, keepdims=True))
                    inv = 1.0 / jnp.sum(e, axis=0, keepdims=True)
                    oh = _dot(vv[h * d:(h + 1) * d], e.astype(BF16))
                    o.append((g[h * d:(h + 1) * d] * (oh * inv)).astype(BF16))
                upd = _tn(jnp.concatenate(o, axis=0), wo[p]) + bo[p]
                zn = (z + upd).astype(BF16)
                zout[row] = zn
                if kind != "last":
                    bout[row] = bias_rows(zn.astype(F32), lnw[p + 1], wb[p + 1])
            rows = pl.ds(i * ROWS, ROWS)
            dst = pl.ds(base * r + i * ROWS, ROWS)
            for s in range(nm):
                u = shifted(base, s)
                target = of(crop, u)
                send(zout.at[rows, pl.ds(pl.multiple_of(u * r, r), r)], zbuf.at[later, dst], zs, zr.at[later], target, kind, s)
                if kind != "last":
                    send(bout.at[rows], bbuf.at[later, dst], bs, br.at[later], target, kind, s)
            return carry
        lax.fori_loop(0, r // ROWS, step, 0)
        drain_sent(zout, zout.at[:, pl.ds(0, n - r)], zs, kind)
        if kind != "last":
            drain_sent(bbuf.at[now], bbuf.at[now, pl.ds(0, n - r)], bs, kind)

    run_pass(0, "first")

    def mid(p, carry):
        run_pass(p, "mid")
        return carry
    lax.fori_loop(1, last, mid, 0)
    run_pass(last, "last")

    end = 2
    drain(zbuf.at[end], zr.at[end])

    def widen(i, carry):
        rows = pl.ds(pl.multiple_of(i * r * r, r * r), r * r)
        zf[rows, :] = zbuf[end, pl.ds(i * r, r)].astype(F32).reshape(r * r, c)
        return carry
    lax.fori_loop(0, n // r, widen, 0)

    def finish(row, carry):
        out[row] = zf[pl.ds(row, n, stride=r), :].astype(BF16)
        return carry
    lax.fori_loop(0, r, finish, 0)


def solution(mesh):
    nd, nm = mesh.shape["data"], mesh.shape["dap"]

    def local(zl, res_mask, ln_w, w_in, b_g, w_b, w_o, b_o):
        r, n, c = zl.shape
        layers, two = w_in.shape[:2]
        m = layers * two
        hd, heads = w_o.shape[2], w_b.shape[3]
        w_in = w_in.reshape(m, c, 4, hd)
        wk = w_in[:, :, 1]
        wt = jnp.concatenate([w_in[:, :, 0], w_in[:, :, 2], w_in[:, :, 3]], axis=-1).swapaxes(1, 2)
        wbt = w_b.reshape(m, c, heads).swapaxes(1, 2)
        wb = jnp.concatenate([wbt, wbt], axis=1)
        bg = jnp.broadcast_to(b_g.astype(F32).reshape(m, hd, 1), (m, hd, LANES))
        maskb = jnp.broadcast_to(jnp.where(res_mask > 0, 0.0, NEG * LOG2E).astype(F32)[:, None], (n, LANES))
        vm = pl.BlockSpec(memory_space=pltpu.VMEM)
        return pl.pallas_call(
            functools.partial(_kernel, nd, nm),
            out_shape=jax.ShapeDtypeStruct((r, n, c), BF16),
            in_specs=[vm] * 9,
            out_specs=vm,
            scratch_shapes=[
                pltpu.VMEM((r, n, c), BF16),
                pltpu.VMEM((r, 2 * heads, LANES), BF16),
                pltpu.VMEM((3, n, r, c), BF16),
                pltpu.VMEM((3, n, 2 * heads, LANES), BF16),
                pltpu.VMEM((n * r, c), F32),
                pltpu.VMEM((n * 2 * heads, LANES), F32),
                pltpu.VMEM((heads, n, n), F32),
                pltpu.VMEM((2, n, LANES), F32),
                pltpu.SemaphoreType.DMA,
                pltpu.SemaphoreType.DMA,
                pltpu.SemaphoreType.DMA((3,)),
                pltpu.SemaphoreType.DMA((3,)),
                pltpu.SemaphoreType.DMA,
                pltpu.SemaphoreType.DMA,
            ],
            compiler_params=pltpu.CompilerParams(collective_id=0, has_side_effects=True, vmem_limit_bytes=56 * 1024 * 1024),
        )(zl, maskb, ln_w.astype(F32).reshape(m, 2, c), wk, wt, bg, wb,
          w_o.reshape(m, hd, c), b_o.astype(F32).reshape(m, 1, c))

    rows = P(('data', 'dap'))
    return jax.shard_map(local, mesh=mesh,
                         in_specs=(rows, P('data'), P(), P(), P(), P(), P(), P()),
                         out_specs=rows, check_vma=False)
```

time: 1490 us -> 732 us (0.49)
  Pallas kernels: 0 us -> 717 us
  matrix products: 440 us -> 0 us
  waiting for transfers between devices: 415 us -> 0 us
  blocking collectives: 301 us -> 0 us
  local copies, waits for them, and re-layouts: 145 us -> 8.58 us
  other arithmetic: 95.7 us -> 3.1 us
  starting transfers between devices: 80.5 us -> 0 us
    pallas_call x0 -> x1, Pallas kernels: none -> 717 us  [local(): pl.pallas_call(functools.partial(_kernel, nd, nm), out_shape=jax.ShapeDty...]
    all_to_all x15 -> x0, waiting for transfers between devices: 415 us -> none  [the longest x8 221 us: local(): zt = lax.all_to_all(zl, 'dap', 1, 0, tiled=True)]
    all_gather x16 -> x0, blocking collectives: 268 us -> none  [_tri_start(): b = lax.all_gather(b.reshape(r, n, -1), 'dap', axis=0, tiled=True)]
    dot_general x112 -> x0, matrix products: 246 us -> none  [the longest x32 146 us: block(): o = jnp.einsum('bhjk,bkhd->bjhd', p, v, preferred_element_type=F32)]
    sub x32 -> x0, matrix products: 193 us -> none  [block(): p = jax.nn.softmax(s, axis=-1).astype(BF16)]
    while x240 -> x0, local copies, waits for them, and re-layouts: 81.3 us -> none
    all_to_all x15 -> x0, starting transfers between devices: 80.5 us -> none  [the longest x8 42 us: local(): zt = lax.all_to_all(zl, 'dap', 1, 0, tiled=True)]
    reduce_sum x96 -> x0, other arithmetic: 62 us -> none  [the longest x48 42.4 us: _ln(): var = jnp.mean(jnp.square(x - mu), axis=-1, keepdims=True)]
  transfers between devices with their start and end apart: 15 -> 0, of which waited for: 15 -> 0; matrix products, arithmetic and copies ran while one was open for 0% -> 0% of each run, Pallas kernels for 0% -> 0%
where the time goes in v1:
time: 732 us; the launch traced here: 729 us
  Pallas kernels  717 us (98%)
  local copies, waits for them, and re-layouts  8.58 us (1%)
    pallas_call x1, Pallas kernels, local(): pl.pallas_call(functools.partial(_kernel, nd, nm), out_shape=jax.ShapeDty...  717 us

profile of v1, /device:TPU:21, one launch (start us, length us, event | category | flops | bytes accessed | tf_op | source)
XLA Modules:
  0.0 728.7 jit_solution(15927095236024212941)
XLA Ops:
  0.0 3.0 copy.10
  3.0 0.1 slice_bitcast_fusion.2
  3.2 0.0 copy-start.2
  3.2 0.0 copy-start.4
  3.2 0.0 copy-start
  3.2 0.0 copy-start.1
  3.2 0.0 copy-start.3
  3.3 1.3 maximum_bitcast_fusion.wt
  4.5 1.0 copy.15
  5.5 0.0 copy-done.2
  5.5 1.3 broadcast_in_dim.29.bg
  6.8 0.0 copy-done.4
  6.9 0.8 broadcast_in_dim.26.maskb
  7.6 0.0 copy-done
  7.6 0.6 pad_maximum_fusion.wb
  8.2 0.0 copy-done.1
  8.2 0.6 bitcast_convert_fusion.lnw
  8.8 0.0 copy-done.3
  8.8 0.6 reshape.32
  9.4 717.0 %shard_map.82 = bf16[16,256,128]{2,1,0:T(8,128)(2,1)} custom-call(bf16[16,256,128]{2,1,0:T(8,128)(2,1)} %zin.1, f32[256,128]{1,0:T(8,128)} %broadcast_in_dim.26.maskb, f32[16,2,128]{2,1,0:T(2,128)} %bitcast_convert_fusion.lnw, bf16[16,128,128]{2,1,0:T(8,128)(2,1)} %bitcast.27, bf16[16,384,128]{2,1,0:T(8,128)(2,1)} %maximum_bitcast_fusion.wt, ...), custom_call_target="tpu_custom_call" | custom-call | tf_op jit(solution)/shard_map/pallas_call | solution.py:276
  726.4 2.3 copy.20
  (1 shorter events, 0.0 us)
Async XLA Ops:
  3.2 2.3 copy-start.2
  3.2 3.6 copy-start.4
  3.2 4.4 copy-start
  3.2 5.0 copy-start.1
  3.2 5.6 copy-start.3

commit v2 on v1

--- a/solution.py
+++ b/solution.py
@@ -15,6 +15,7 @@
 BF16 = jnp.bfloat16
 MESH = pl.DeviceIdType.MESH
 LANES = 128
+LOOK = 3
 ROWS = 4
 
 
@@ -192,7 +193,7 @@
 
         def step(i, carry):
             w = lnw[p]
-            zs_, ys, ks, qvs, os = [], [], [], [], []
+            zrows, keys, queries, values, gates = [], [], [], [], []
             for q in range(ROWS):
                 row = i * ROWS + q
                 if kind == "first":
@@ -200,26 +201,41 @@
                 else:
                     z = zf[pl.ds(row, n, stride=r), :]
                 y = _ln(z, w)
-                k = _dot(y, wk[p]).astype(BF16)
                 qvt = _nt(wt[p], y)
-                qq = qvt[:hd].astype(BF16)
-                vv = qvt[hd:2 * hd].astype(BF16)
-                t = qvt[2 * hd:] + jnp.concatenate([bg[p], bg[p]], axis=1)
-                g = jax.nn.sigmoid(t)
-                o = []
-                for h in range(heads):
-                    parts = [jnp.zeros((d, n), BF16)] * heads
-                    parts[h] = qq[h * d:(h + 1) * d]
-                    sc = _dot(k, jnp.concatenate(parts, axis=0)) * scale + bias[h]
+                zrows.append(z)
+                keys.append(_dot(y, wk[p]).astype(BF16))
+                queries.append(qvt[:hd].astype(BF16))
+                values.append(qvt[hd:2 * hd].astype(BF16))
+                gates.append(jax.nn.sigmoid(qvt[2 * hd:] + jnp.concatenate([bg[p], bg[p]], axis=1)))
+
+            def scores(q, h):
+                parts = [jnp.zeros((d, n), BF16)] * heads
+                parts[h] = queries[q][h * d:(h + 1) * d]
+                return _dot(keys[q], jnp.concatenate(parts, axis=0))
+
+            units = [(q, h) for q in range(ROWS) for h in range(heads)]
+            raw = [scores(*units[j]) for j in range(LOOK)]
+            outs = []
+            for j, (q, h) in enumerate(units):
+                if j + LOOK < len(units):
+                    raw.append(scores(*units[j + LOOK]))
+                es, invs = [], []
+                for cols in (slice(0, LANES), slice(LANES, 2 * LANES)):
+                    sc = raw[j][:, cols] * scale + bias[h, :, cols]
                     e = jnp.exp2(sc - jnp.max(sc, axis=0, keepdims=True))
-                    inv = 1.0 / jnp.sum(e, axis=0, keepdims=True)
-                    oh = _dot(vv[h * d:(h + 1) * d], e.astype(BF16))
-                    o.append((g[h * d:(h + 1) * d] * (oh * inv)).astype(BF16))
-                upd = _tn(jnp.concatenate(o, axis=0), wo[p]) + bo[p]
-                zn = (z + upd).astype(BF16)
-                zout[row] = zn
-                if kind != "last":
-                    bout[row] = bias_rows(zn.astype(F32), lnw[p + 1], wb[p + 1])
+                    invs.append(1.0 / jnp.sum(e, axis=0, keepdims=True))
+                    es.append(e.astype(BF16))
+                span = slice(h * d, (h + 1) * d)
+                oh = _dot(values[q][span], jnp.concatenate(es, axis=1)) * jnp.concatenate(invs, axis=1)
+                outs.append((gates[q][span] * oh).astype(BF16))
+            news = []
+            for q in range(ROWS):
+                upd = _tn(jnp.concatenate(outs[q * heads:(q + 1) * heads], axis=0), wo[p]) + bo[p]
+                news.append((zrows[q] + upd).astype(BF16))
+                zout[i * ROWS + q] = news[q]
+            if kind != "last":
+                for q in range(ROWS):
+                    bout[i * ROWS + q] = bias_rows(news[q].astype(F32), lnw[p + 1], wb[p + 1])
             rows = pl.ds(i * ROWS, ROWS)
             dst = pl.ds(base * r + i * ROWS, ROWS)
             for s in range(nm):

time: 732 us -> 503 us (0.69)
  Pallas kernels: 717 us -> 491 us
    pallas_call x1, Pallas kernels: 717 us -> 491 us  [local(): pl.pallas_call(functools.partial(_kernel, nd, nm), out_shape=jax.ShapeDty...]
where the time goes in v2:
time: 503 us
  Pallas kernels  491 us (98%)
  local copies, waits for them, and re-layouts  8.58 us (2%)
    pallas_call x1, Pallas kernels, local(): pl.pallas_call(functools.partial(_kernel, nd, nm), out_shape=jax.ShapeDty...  491 us

profile of v2, /device:TPU:21, one launch (start us, length us, event | category | flops | bytes accessed | tf_op | source)
XLA Modules:
  0.0 502.5 jit_solution(16017017875410567915)
XLA Ops:
  0.0 3.0 copy.10
  3.0 0.1 slice_bitcast_fusion.2
  3.2 0.0 copy-start.2
  3.2 0.0 copy-start.4
  3.2 0.0 copy-start
  3.2 0.0 copy-start.1
  3.2 0.0 copy-start.3
  3.3 1.3 maximum_bitcast_fusion.wt
  4.5 1.0 copy.15
  5.5 0.0 copy-done.2
  5.5 1.3 broadcast_in_dim.29.bg
  6.8 0.0 copy-done.4
  6.9 0.8 broadcast_in_dim.26.maskb
  7.6 0.0 copy-done
  7.6 0.6 pad_maximum_fusion.wb
  8.2 0.0 copy-done.1
  8.2 0.6 bitcast_convert_fusion.lnw
  8.8 0.0 copy-done.3
  8.8 0.6 reshape.32
  9.4 490.8 %shard_map.82 = bf16[16,256,128]{2,1,0:T(8,128)(2,1)} custom-call(bf16[16,256,128]{2,1,0:T(8,128)(2,1)} %zin.1, f32[256,128]{1,0:T(8,128)} %broadcast_in_dim.26.maskb, f32[16,2,128]{2,1,0:T(2,128)} %bitcast_convert_fusion.lnw, bf16[16,128,128]{2,1,0:T(8,128)(2,1)} %bitcast.27, bf16[16,384,128]{2,1,0:T(8,128)(2,1)} %maximum_bitcast_fusion.wt, ...), custom_call_target="tpu_custom_call" | custom-call | tf_op jit(solution)/shard_map/pallas_call | solution.py:292
  500.2 2.3 copy.20
  (1 shorter events, 0.0 us)
Async XLA Ops:
  3.2 2.3 copy-start.2
  3.2 3.6 copy-start.4
  3.2 4.4 copy-start
  3.2 5.0 copy-start.1
  3.2 5.6 %copy-start.3 = (bf16[8,2,128]{2,1,0:T(2,128)(2,1)S(1)}, bf16[8,2,128]{2,1,0:T(2,128)(2,1)}, u32[]{:S(2)}) copy-start(bf16[8,2,128]{2,1,0:T(2,128)(2,1)} %param.15) | copy-start | bytes 12292

commit v3 on v2

--- a/solution.py
+++ b/solution.py
@@ -16,7 +16,10 @@
 MESH = pl.DeviceIdType.MESH
 LANES = 128
 LOOK = 3
-ROWS = 4
+AHEAD = 2
+ROWS = 8
+CHUNK = 2
+EDGE_ROWS = 4
 
 
 def _ln(x, w):
@@ -40,7 +43,7 @@
 
 def _kernel(nd, nm, zin, maskb, lnw, wk, wt, bg, wb, wo, bo, out,
             zout, bout, zbuf, bbuf, zf, bf, bias, mbuf,
-            zs, bs, zr, br, ms, mr):
+            zs, bs, fs, zr, br, fr, ms, mr):
     r, n, c = zin.shape
     passes, hd = wk.shape[0], wk.shape[2]
     heads = wb.shape[1] // 2
@@ -105,6 +108,19 @@
             pl.when(inside)(lambda: drain(ref_less, sem))
             pl.when(jnp.logical_not(inside))(lambda: drain(ref_all, sem))
 
+    core = me_p % 2
+
+    def hand_on(slot_):
+        half = bbuf.at[slot_, :, core]
+        drain(half, br.at[slot_])
+        pltpu.make_async_remote_copy(half, half, fs, fr.at[slot_], device_id=(me_d, me_p + 1 - 2 * core),
+                                     device_id_type=MESH).start()
+
+    def handed_on(slot_):
+        half = bbuf.at[slot_, :, core]
+        drain(half, fr.at[slot_])
+        drain(half, fs)
+
     barrier = pltpu.get_barrier_semaphore()
     groups = [(home_of, low), (cube_of, mine)] + ([(cube_of, low), (home_of, mine)] if cube else [])
     if not cube:
@@ -147,16 +163,17 @@
 
     def first_bias(i, carry):
         w = lnw[0]
-        for q in range(ROWS):
-            row = i * ROWS + q
+        for q in range(EDGE_ROWS):
+            row = i * EDGE_ROWS + q
             bout[row] = bias_rows(zin[row].astype(F32), w, wb[0])
         return carry
-    lax.fori_loop(0, r // ROWS, first_bias, 0)
-    for s in range(nm):
+    lax.fori_loop(0, r // EDGE_ROWS, first_bias, 0)
+    for s in range(0, nm, 2):
         u = shifted(me_p, s)
-        send(bout, bbuf.at[2, pl.ds(me_p * r, r)], bs, br.at[2], home_of(low, u), "mid", s)
-    drain(bbuf.at[2], br.at[2])
-    drain(bbuf.at[2, pl.ds(0, n - r)], bs)
+        send(bout, bbuf.at[2, me_p // 2, core], bs, br.at[2], home_of(low, u), "mid", s)
+    hand_on(2)
+    drain(bbuf.at[2, pl.ds(0, nm // 2 - 1), core], bs)
+    handed_on(2)
     if cube:
         pl.when(jnp.logical_not(me_m))(lambda: drain(maskb, ms))
     drain(mbuf.at[1], mr)
@@ -165,18 +182,19 @@
         now = 2 if kind == "first" else p % 2
         later = 2 if kind == "last" else (p + 1) % 2
         if kind != "first":
+            hand_on(now)
             drain(zbuf.at[now], zr.at[now])
-            drain(bbuf.at[now], br.at[now])
 
             def widen(i, carry):
                 rows = pl.ds(pl.multiple_of(i * r * r, r * r), r * r)
                 zf[rows, :] = zbuf[now, pl.ds(i * r, r)].astype(F32).reshape(r * r, c)
                 return carry
             lax.fori_loop(0, n // r, widen, 0)
+            handed_on(now)
 
         def widen_bias(i, carry):
             rows = pl.ds(pl.multiple_of(i * r * 2 * heads, r * 2 * heads), r * 2 * heads)
-            bf[rows, :] = bbuf[now, pl.ds(i * r, r)].astype(F32).reshape(r * 2 * heads, LANES)
+            bf[rows, :] = bbuf[now, i // 2, i % 2].astype(F32).reshape(r * 2 * heads, LANES)
             return carry
         lax.fori_loop(0, n // r, widen_bias, 0)
         mask = mbuf.at[0 if kind == "first" else 1]
@@ -191,32 +209,56 @@
         base = me_p if kind == "first" else slot
         of = home_of if kind == "last" else cube_of
 
-        def step(i, carry):
+        def post(first_row, count):
+            rows = pl.ds(first_row, count)
+            for s in range(nm):
+                u = shifted(base, s)
+                target = of(crop, u)
+                if kind != "last" and s % 2 == 0:
+                    send(bout.at[rows], bbuf.at[later, base // 2, core, rows], bs, br.at[later], target, kind, s)
+                send(zout.at[rows, pl.ds(pl.multiple_of(u * r, r), r)],
+                     zbuf.at[later, pl.ds(base * r + first_row, count)], zs, zr.at[later], target, kind, s)
+
+        def attend(first_row, count, chunk):
             w = lnw[p]
-            zrows, keys, queries, values, gates = [], [], [], [], []
-            for q in range(ROWS):
-                row = i * ROWS + q
-                if kind == "first":
-                    z = zin[row].astype(F32)
-                else:
-                    z = zf[pl.ds(row, n, stride=r), :]
+            gate_b = jnp.concatenate([bg[p], bg[p]], axis=1)
+            zrows, keys, queries, values, gates, raw, outs, news = [], [], [], [], [], [], [], []
+            units = [(q, h) for q in range(count) for h in range(heads)]
+
+            def project(q):
+                row = first_row + q
+                z = zin[row].astype(F32) if kind == "first" else zf[pl.ds(row, n, stride=r), :]
                 y = _ln(z, w)
                 qvt = _nt(wt[p], y)
                 zrows.append(z)
                 keys.append(_dot(y, wk[p]).astype(BF16))
                 queries.append(qvt[:hd].astype(BF16))
                 values.append(qvt[hd:2 * hd].astype(BF16))
-                gates.append(jax.nn.sigmoid(qvt[2 * hd:] + jnp.concatenate([bg[p], bg[p]], axis=1)))
+                gates.append(jax.nn.sigmoid(qvt[2 * hd:] + gate_b))
 
             def scores(q, h):
                 parts = [jnp.zeros((d, n), BF16)] * heads
                 parts[h] = queries[q][h * d:(h + 1) * d]
                 return _dot(keys[q], jnp.concatenate(parts, axis=0))
 
-            units = [(q, h) for q in range(ROWS) for h in range(heads)]
-            raw = [scores(*units[j]) for j in range(LOOK)]
-            outs = []
+            def update(q):
+                upd = _tn(jnp.concatenate(outs[q * heads:(q + 1) * heads], axis=0), wo[p]) + bo[p]
+                news.append((zrows[q] + upd).astype(BF16))
+                zout[first_row + q] = news[q]
+
+            def finish_row(q):
+                if kind != "last":
+                    bout[first_row + q] = bias_rows(news[q].astype(F32), lnw[p + 1], wb[p + 1])
+                if (q + 1) % chunk == 0:
+                    post(first_row + q + 1 - chunk, chunk)
+
+            for q in range(min(AHEAD, count)):
+                project(q)
+            for j in range(LOOK):
+                raw.append(scores(*units[j]))
             for j, (q, h) in enumerate(units):
+                if h == 0 and q + AHEAD < count:
+                    project(q + AHEAD)
                 if j + LOOK < len(units):
                     raw.append(scores(*units[j + LOOK]))
                 es, invs = [], []
@@ -228,27 +270,22 @@
                 span = slice(h * d, (h + 1) * d)
                 oh = _dot(values[q][span], jnp.concatenate(es, axis=1)) * jnp.concatenate(invs, axis=1)
                 outs.append((gates[q][span] * oh).astype(BF16))
-            news = []
-            for q in range(ROWS):
-                upd = _tn(jnp.concatenate(outs[q * heads:(q + 1) * heads], axis=0), wo[p]) + bo[p]
-                news.append((zrows[q] + upd).astype(BF16))
-                zout[i * ROWS + q] = news[q]
-            if kind != "last":
-                for q in range(ROWS):
-                    bout[i * ROWS + q] = bias_rows(news[q].astype(F32), lnw[p + 1], wb[p + 1])
-            rows = pl.ds(i * ROWS, ROWS)
-            dst = pl.ds(base * r + i * ROWS, ROWS)
-            for s in range(nm):
-                u = shifted(base, s)
-                target = of(crop, u)
-                send(zout.at[rows, pl.ds(pl.multiple_of(u * r, r), r)], zbuf.at[later, dst], zs, zr.at[later], target, kind, s)
-                if kind != "last":
-                    send(bout.at[rows], bbuf.at[later, dst], bs, br.at[later], target, kind, s)
+                if h == 1 and q > 0:
+                    update(q - 1)
+                if h == 3 and q > 0:
+                    finish_row(q - 1)
+            update(count - 1)
+            finish_row(count - 1)
+
+        block, chunk = (ROWS, CHUNK) if kind == "mid" else (EDGE_ROWS, EDGE_ROWS)
+
+        def step(i, carry):
+            attend(i * block, block, chunk)
             return carry
-        lax.fori_loop(0, r // ROWS, step, 0)
+        lax.fori_loop(0, r // block, step, 0)
         drain_sent(zout, zout.at[:, pl.ds(0, n - r)], zs, kind)
         if kind != "last":
-            drain_sent(bbuf.at[now], bbuf.at[now, pl.ds(0, n - r)], bs, kind)
+            drain_sent(bbuf.at[now, :, core], bbuf.at[now, pl.ds(0, nm // 2 - 1), core], bs, kind)
 
     run_pass(0, "first")
 
@@ -298,13 +335,15 @@
                 pltpu.VMEM((r, n, c), BF16),
                 pltpu.VMEM((r, 2 * heads, LANES), BF16),
                 pltpu.VMEM((3, n, r, c), BF16),
-                pltpu.VMEM((3, n, 2 * heads, LANES), BF16),
+                pltpu.VMEM((3, nm // 2, 2, r, 2 * heads, LANES), BF16),
                 pltpu.VMEM((n * r, c), F32),
                 pltpu.VMEM((n * 2 * heads, LANES), F32),
                 pltpu.VMEM((heads, n, n), F32),
                 pltpu.VMEM((2, n, LANES), F32),
                 pltpu.SemaphoreType.DMA,
                 pltpu.SemaphoreType.DMA,
+                pltpu.SemaphoreType.DMA,
+                pltpu.SemaphoreType.DMA((3,)),
                 pltpu.SemaphoreType.DMA((3,)),
                 pltpu.SemaphoreType.DMA((3,)),
                 pltpu.SemaphoreType.DMA,

time: 503 us -> 467 us (0.928)
  Pallas kernels: 491 us -> 451 us
    pallas_call x1, Pallas kernels: 491 us -> 451 us  [local(): pl.pallas_call(functools.partial(_kernel, nd, nm), out_shape=jax.ShapeDty...]
where the time goes in v3:
time: 467 us; the launch traced here: 462 us
  Pallas kernels  451 us (97%)
  local copies, waits for them, and re-layouts  8.58 us (2%)
    pallas_call x1, Pallas kernels, local(): pl.pallas_call(functools.partial(_kernel, nd, nm), out_shape=jax.ShapeDty...  451 us

profile of v3, /device:TPU:21, one launch (start us, length us, event | category | flops | bytes accessed | tf_op | source)
XLA Modules:
  0.0 462.3 jit_solution(18434816092576726921)
XLA Ops:
  0.0 3.0 copy.10
  3.0 0.1 slice_bitcast_fusion.2
  3.2 0.0 copy-start.2
  3.2 0.0 copy-start.4
  3.2 0.0 copy-start
  3.2 0.0 copy-start.1
  3.2 0.0 copy-start.3
  3.3 1.3 maximum_bitcast_fusion.wt
  4.5 1.0 copy.15
  5.5 0.0 copy-done.2
  5.5 1.3 broadcast_in_dim.29.bg
  6.8 0.0 copy-done.4
  6.9 0.8 broadcast_in_dim.26.maskb
  7.6 0.0 copy-done
  7.6 0.6 pad_maximum_fusion.wb
  8.2 0.0 copy-done.1
  8.2 0.6 bitcast_convert_fusion.lnw
  8.8 0.0 copy-done.3
  8.8 0.6 reshape.32
  9.4 450.5 %shard_map.82 = bf16[16,256,128]{2,1,0:T(8,128)(2,1)} custom-call(bf16[16,256,128]{2,1,0:T(8,128)(2,1)} %zin.1, f32[256,128]{1,0:T(8,128)} %broadcast_in_dim.26.maskb, f32[16,2,128]{2,1,0:T(2,128)} %bitcast_convert_fusion.lnw, bf16[16,128,128]{2,1,0:T(8,128)(2,1)} %bitcast.27, bf16[16,384,128]{2,1,0:T(8,128)(2,1)} %maximum_bitcast_fusion.wt, ...), custom_call_target="tpu_custom_call" | custom-call | tf_op jit(solution)/shard_map/pallas_call | solution.py:329
  460.0 2.3 copy.20
  (1 shorter events, 0.0 us)
Async XLA Ops:
  3.2 2.3 copy-start.2
  3.2 3.6 copy-start.4
  3.2 4.4 copy-start
  3.2 5.0 %copy-start.1 = (bf16[8,2,2,128]{3,2,1,0:T(2,128)(2,1)S(1)}, bf16[8,2,2,128]{3,2,1,0:T(2,128)(2,1)}, u32[]{:S(2)}) copy-start(bf16[8,2,2,128]{3,2,1,0:T(2,128)(2,1)} %param.10) | copy-start | bytes 24580
  3.2 5.6 %copy-start.3 = (bf16[8,2,128]{2,1,0:T(2,128)(2,1)S(1)}, bf16[8,2,128]{2,1,0:T(2,128)(2,1)}, u32[]{:S(2)}) copy-start(bf16[8,2,128]{2,1,0:T(2,128)(2,1)} %param.15) | copy-start | bytes 12292

commit v4 on v3

--- a/solution.py
+++ b/solution.py
@@ -41,11 +41,11 @@
     return jnp.dot(a, b, preferred_element_type=F32)
 
 
-def _kernel(nd, nm, zin, maskb, lnw, wk, wt, bg, wb, wo, bo, out,
-            zout, bout, zbuf, bbuf, zf, bf, bias, mbuf,
-            zs, bs, fs, zr, br, fr, ms, mr):
+def _kernel(nd, nm, zin, maskb, small, win, wb, wo, out,
+            zout, bout, zbuf, bbuf, zf, bf, bias, mbuf, wt, zrelay, brelay,
+            zs, bs, fs, zr, br, fr, ms, mr, rs, zrr, brr):
     r, n, c = zin.shape
-    passes, hd = wk.shape[0], wk.shape[2]
+    passes, hd = wo.shape[0], wo.shape[1]
     heads = wb.shape[1] // 2
     d = hd // heads
     last = passes - 1
@@ -76,6 +76,8 @@
 
         cube_of = home_of
 
+    hslot = me_p
+
     def is_me(t):
         return jnp.logical_and(t[0] == me_d, t[1] == me_p)
 
@@ -102,7 +104,7 @@
         pltpu.make_async_copy(ref, ref, sem).wait()
 
     def drain_sent(ref_all, ref_less, sem, kind):
-        if kind == "mid" or not cube:
+        if kind != "last" or not cube:
             drain(ref_less, sem)
         else:
             pl.when(inside)(lambda: drain(ref_less, sem))
@@ -135,13 +137,16 @@
             return carry
         lax.fori_loop(0, nm, greet, 0)
     if cube:
+        for s in range(1, 4):
+            pl.semaphore_signal(barrier, inc=1, device_id=home_of((low + s) % 4, me_p), device_id_type=MESH)
+
         @pl.when(inside)
         def _():
-            pl.semaphore_wait(barrier, 4 * (nm - 1))
+            pl.semaphore_wait(barrier, 4 * (nm - 1) + 3)
 
         @pl.when(jnp.logical_not(inside))
         def _():
-            pl.semaphore_wait(barrier, 2 * (nm - 1) + 2 * nm)
+            pl.semaphore_wait(barrier, 2 * (nm - 1) + 2 * nm + 3)
     else:
         pl.semaphore_wait(barrier, nm - 1)
 
@@ -151,32 +156,37 @@
         b = _nt(wbw, _ln(z, w))
         return jnp.where(low_half, b[:, :LANES], b[:, LANES:]).astype(BF16)
 
-    mbuf[0] = maskb[...]
-    mt = cube_of(low, me_p)
+    mt = cube_of(low, hslot)
     if cube:
         me_m = is_me(mt)
-        pl.when(me_m)(lambda: pltpu.make_async_copy(maskb, mbuf.at[1], mr).start())
+        pl.when(me_m)(lambda: pltpu.make_async_copy(maskb, mbuf, mr).start())
         pl.when(jnp.logical_not(me_m))(lambda: pltpu.make_async_remote_copy(
-            maskb, mbuf.at[1], ms, mr, device_id=mt, device_id_type=MESH).start())
+            maskb, mbuf, ms, mr, device_id=mt, device_id_type=MESH).start())
     else:
-        pltpu.make_async_copy(maskb, mbuf.at[1], mr).start()
+        pltpu.make_async_copy(maskb, mbuf, mr).start()
 
     def first_bias(i, carry):
-        w = lnw[0]
+        w = small[0]
         for q in range(EDGE_ROWS):
             row = i * EDGE_ROWS + q
             bout[row] = bias_rows(zin[row].astype(F32), w, wb[0])
         return carry
     lax.fori_loop(0, r // EDGE_ROWS, first_bias, 0)
     for s in range(0, nm, 2):
-        u = shifted(me_p, s)
-        send(bout, bbuf.at[2, me_p // 2, core], bs, br.at[2], home_of(low, u), "mid", s)
+        u = shifted(hslot, s)
+        send(bout, bbuf.at[2, hslot // 2, core], bs, br.at[2], home_of(low, u), "mid", s)
+
+    def turn(i, carry):
+        for t, part in enumerate((0, 2, 3)):
+            wt[i, t * hd:(t + 1) * hd] = win[i, :, part * hd:(part + 1) * hd].T
+        return carry
+    lax.fori_loop(0, passes, turn, 0)
     hand_on(2)
     drain(bbuf.at[2, pl.ds(0, nm // 2 - 1), core], bs)
     handed_on(2)
     if cube:
         pl.when(jnp.logical_not(me_m))(lambda: drain(maskb, ms))
-    drain(mbuf.at[1], mr)
+    drain(mbuf, mr)
 
     def run_pass(p, kind):
         now = 2 if kind == "first" else p % 2
@@ -197,16 +207,17 @@
             bf[rows, :] = bbuf[now, i // 2, i % 2].astype(F32).reshape(r * 2 * heads, LANES)
             return carry
         lax.fori_loop(0, n // r, widen_bias, 0)
-        mask = mbuf.at[0 if kind == "first" else 1]
+        mask_row = (maskb if kind == "first" else mbuf)[...]
+        mask = jnp.concatenate([jnp.broadcast_to(mask_row[t:t + 1], (LANES, LANES)).T for t in range(n // LANES)], axis=0)
         for h in range(heads):
             halves = [bf[pl.ds(half * heads + h, n, stride=2 * heads), :] * LOG2E for half in range(2)]
             if kind == "first":
                 halves = jnp.split(jnp.concatenate(halves, axis=1).T, 2, axis=1)
             for half in range(2):
-                bias[h, :, half * LANES:(half + 1) * LANES] = halves[half] + mask[...]
+                bias[h, :, half * LANES:(half + 1) * LANES] = halves[half] + mask
 
         crop = low if kind == "first" else mine
-        base = me_p if kind == "first" else slot
+        base = hslot if kind == "first" else slot
         of = home_of if kind == "last" else cube_of
 
         def post(first_row, count):
@@ -219,9 +230,33 @@
                 send(zout.at[rows, pl.ds(pl.multiple_of(u * r, r), r)],
                      zbuf.at[later, pl.ds(base * r + first_row, count)], zs, zr.at[later], target, kind, s)
 
+        def spread(i, count):
+            rows = pl.ds(i * count, count)
+            for s in range(4):
+                lo = (low + s) % 4
+                cols = pl.ds(pl.multiple_of(lo * sub * r, r), sub * r)
+                target = home_of(lo, me_p)
+                send(bout.at[rows], brelay.at[low, rows], rs.at[0], brr.at[i], target, "mid", s)
+                send(zout.at[rows, cols], zrelay.at[low, rows], rs.at[1], zrr.at[i], target, "mid", s)
+
+        def relay(i, count):
+            rows = pl.ds(i * count, count)
+            drain(brelay.at[:, rows], brr.at[i])
+            drain(zrelay.at[:, rows], zrr.at[i])
+            for s in range(nm):
+                u = shifted(me_p, s)
+                to = u // sub
+                if s % 2 == 0:
+                    send(brelay.at[to, rows], bbuf.at[later, me_p // 2, core, rows], bs, br.at[later], (me_d, u), "mid", s)
+                cols = pl.ds(pl.multiple_of((u % sub) * r, r), r)
+                send(zrelay.at[to, rows, cols], zbuf.at[later, pl.ds(me_p * r + i * count, count)],
+                     zs, zr.at[later], (me_d, u), "mid", s)
+
         def attend(first_row, count, chunk):
-            w = lnw[p]
-            gate_b = jnp.concatenate([bg[p], bg[p]], axis=1)
+            par = small[p]
+            w = par[0:2]
+            out_b = par[3:4]
+            gate_b = jnp.broadcast_to(par[2:3], (n, hd)).T
             zrows, keys, queries, values, gates, raw, outs, news = [], [], [], [], [], [], [], []
             units = [(q, h) for q in range(count) for h in range(heads)]
 
@@ -231,7 +266,7 @@
                 y = _ln(z, w)
                 qvt = _nt(wt[p], y)
                 zrows.append(z)
-                keys.append(_dot(y, wk[p]).astype(BF16))
+                keys.append(_dot(y, win[p, :, hd:2 * hd]).astype(BF16))
                 queries.append(qvt[:hd].astype(BF16))
                 values.append(qvt[hd:2 * hd].astype(BF16))
                 gates.append(jax.nn.sigmoid(qvt[2 * hd:] + gate_b))
@@ -242,14 +277,14 @@
                 return _dot(keys[q], jnp.concatenate(parts, axis=0))
 
             def update(q):
-                upd = _tn(jnp.concatenate(outs[q * heads:(q + 1) * heads], axis=0), wo[p]) + bo[p]
+                upd = _tn(jnp.concatenate(outs[q * heads:(q + 1) * heads], axis=0), wo[p]) + out_b
                 news.append((zrows[q] + upd).astype(BF16))
                 zout[first_row + q] = news[q]
 
             def finish_row(q):
                 if kind != "last":
-                    bout[first_row + q] = bias_rows(news[q].astype(F32), lnw[p + 1], wb[p + 1])
-                if (q + 1) % chunk == 0:
+                    bout[first_row + q] = bias_rows(news[q].astype(F32), small[p + 1], wb[p + 1])
+                if (q + 1) % chunk == 0 and not (cube and kind == "first"):
                     post(first_row + q + 1 - chunk, chunk)
 
             for q in range(min(AHEAD, count)):
@@ -281,8 +316,15 @@
 
         def step(i, carry):
             attend(i * block, block, chunk)
+            if cube and kind == "first":
+                spread(i, block)
+                pl.when(i > 0)(lambda: relay(i - 1, block))
             return carry
         lax.fori_loop(0, r // block, step, 0)
+        if cube and kind == "first":
+            relay(r // block - 1, block)
+            drain(zrelay.at[pl.ds(0, 3)], rs.at[1])
+            drain(brelay.at[pl.ds(0, 3)], rs.at[0])
         drain_sent(zout, zout.at[:, pl.ds(0, n - r)], zs, kind)
         if kind != "last":
             drain_sent(bbuf.at[now, :, core], bbuf.at[now, pl.ds(0, nm // 2 - 1), core], bs, kind)
@@ -318,18 +360,16 @@
         layers, two = w_in.shape[:2]
         m = layers * two
         hd, heads = w_o.shape[2], w_b.shape[3]
-        w_in = w_in.reshape(m, c, 4, hd)
-        wk = w_in[:, :, 1]
-        wt = jnp.concatenate([w_in[:, :, 0], w_in[:, :, 2], w_in[:, :, 3]], axis=-1).swapaxes(1, 2)
         wbt = w_b.reshape(m, c, heads).swapaxes(1, 2)
         wb = jnp.concatenate([wbt, wbt], axis=1)
-        bg = jnp.broadcast_to(b_g.astype(F32).reshape(m, hd, 1), (m, hd, LANES))
-        maskb = jnp.broadcast_to(jnp.where(res_mask > 0, 0.0, NEG * LOG2E).astype(F32)[:, None], (n, LANES))
+        small = jnp.concatenate([ln_w, b_g[:, :, None], b_o[:, :, None]], axis=2).astype(F32).reshape(m, 4, c)
+        maskb = jnp.where(res_mask > 0, 0.0, NEG * LOG2E).astype(F32).reshape(n // LANES, LANES)
+        maskb = jnp.pad(maskb, ((0, 8 - n // LANES), (0, 0)))
         vm = pl.BlockSpec(memory_space=pltpu.VMEM)
         return pl.pallas_call(
             functools.partial(_kernel, nd, nm),
             out_shape=jax.ShapeDtypeStruct((r, n, c), BF16),
-            in_specs=[vm] * 9,
+            in_specs=[vm] * 6,
             out_specs=vm,
             scratch_shapes=[
                 pltpu.VMEM((r, n, c), BF16),
@@ -339,7 +379,10 @@
                 pltpu.VMEM((n * r, c), F32),
                 pltpu.VMEM((n * 2 * heads, LANES), F32),
                 pltpu.VMEM((heads, n, n), F32),
-                pltpu.VMEM((2, n, LANES), F32),
+                pltpu.VMEM((8, LANES), F32),
+                pltpu.VMEM((m, 3 * hd, c), BF16),
+                pltpu.VMEM((4, r, n // 4, c), BF16),
+                pltpu.VMEM((4, r, 2 * heads, LANES), BF16),
                 pltpu.SemaphoreType.DMA,
                 pltpu.SemaphoreType.DMA,
                 pltpu.SemaphoreType.DMA,
@@ -348,10 +391,12 @@
                 pltpu.SemaphoreType.DMA((3,)),
                 pltpu.SemaphoreType.DMA,
                 pltpu.SemaphoreType.DMA,
+                pltpu.SemaphoreType.DMA((2,)),
+                pltpu.SemaphoreType.DMA((r // EDGE_ROWS,)),
+                pltpu.SemaphoreType.DMA((r // EDGE_ROWS,)),
             ],
             compiler_params=pltpu.CompilerParams(collective_id=0, has_side_effects=True, vmem_limit_bytes=56 * 1024 * 1024),
-        )(zl, maskb, ln_w.astype(F32).reshape(m, 2, c), wk, wt, bg, wb,
-          w_o.reshape(m, hd, c), b_o.astype(F32).reshape(m, 1, c))
+        )(zl, maskb, small, w_in.reshape(m, c, 4 * hd), wb, w_o.reshape(m, hd, c))
 
     rows = P(('data', 'dap'))
     return jax.shard_map(local, mesh=mesh,

time: 467 us -> 408 us (0.87)
  Pallas kernels: 451 us -> 400 us
    pallas_call x1, Pallas kernels: 451 us -> 400 us  [local(): pl.pallas_call(functools.partial(_kernel, nd, nm), out_shape=jax.ShapeDty...]
where the time goes in v4:
time: 408 us; the launch traced here: 407 us
  Pallas kernels  400 us (98%)
  local copies, waits for them, and re-layouts  4.28 us (1%)
    pallas_call x1, Pallas kernels, local(): pl.pallas_call(functools.partial(_kernel, nd, nm), out_shape=jax.ShapeDty...  400 us

profile of v4, /device:TPU:21, one launch (start us, length us, event | category | flops | bytes accessed | tf_op | source)
XLA Modules:
  0.0 407.4 jit_solution(1470331131985891754)
XLA Ops:
  0.0 0.7 fusion
  0.7 0.6 pad.4.maskb
  1.3 0.7 copy.9
  2.0 0.7 copy.10
  2.7 1.3 maximum_convert_fusion.small
  4.0 1.4 pad_maximum_fusion.wb
  5.4 399.6 %shard_map.82 = bf16[16,256,128]{2,1,0:T(8,128)(2,1)} custom-call(bf16[16,256,128]{2,1,0:T(8,128)(2,1)} %zin.1, f32[8,128]{1,0:T(8,128)} %pad.4.maskb, f32[16,4,128]{2,1,0:T(4,128)} %maximum_convert_fusion.small, bf16[16,128,512]{2,1,0:T(8,128)(2,1)} %bitcast.10, bf16[16,8,128]{2,1,0:T(8,128)(2,1)} %pad_maximum_fusion.wb, bf16[16,128,128]{2,1,0:T(8,128)(2,1)} %bitcast.11), custom_call_target="tpu_custom_call" | custom-call | tf_op jit(solution)/shard_map/pallas_call | solution.py:369
  405.1 2.3 copy.12

commit v5 on v4

--- a/solution.py
+++ b/solution.py
@@ -17,8 +17,9 @@
 LANES = 128
 LOOK = 3
 AHEAD = 2
-ROWS = 8
-CHUNK = 2
+ROWS = 4
+CHUNKS = (2, 4)
+BIAS_ROWS = 4
 EDGE_ROWS = 4
 
 
@@ -42,7 +43,7 @@
 
 
 def _kernel(nd, nm, zin, maskb, small, win, wb, wo, out,
-            zout, bout, zbuf, bbuf, zf, bf, bias, mbuf, wt, zrelay, brelay,
+            zout, bout, zbuf, bbuf, zf, bf, bias, mbuf, wt, gt, masks, zrelay, brelay,
             zs, bs, fs, zr, br, fr, ms, mr, rs, zrr, brr):
     r, n, c = zin.shape
     passes, hd = wo.shape[0], wo.shape[1]
@@ -77,6 +78,11 @@
         cube_of = home_of
 
     hslot = me_p
+    if cube:
+        lows = [(low + a) % 4 for a in range(4)]
+        places = [(me_p % sub + b) % sub for b in range(sub)]
+        lines = [home_of(lo, me_p)[0] for lo in lows]
+        stretch = [mine * sub + b for b in places]
 
     def is_me(t):
         return jnp.logical_and(t[0] == me_d, t[1] == me_p)
@@ -177,6 +183,7 @@
         send(bout, bbuf.at[2, hslot // 2, core], bs, br.at[2], home_of(low, u), "mid", s)
 
     def turn(i, carry):
+        gt[i] = jnp.broadcast_to(small[i][2:3], (LANES, hd)).T
         for t, part in enumerate((0, 2, 3)):
             wt[i, t * hd:(t + 1) * hd] = win[i, :, part * hd:(part + 1) * hd].T
         return carry
@@ -187,6 +194,9 @@
     if cube:
         pl.when(jnp.logical_not(me_m))(lambda: drain(maskb, ms))
     drain(mbuf, mr)
+    for k, ref in enumerate((maskb, mbuf)):
+        row = ref[...]
+        masks[k] = jnp.concatenate([jnp.broadcast_to(row[t:t + 1], (LANES, LANES)).T for t in range(n // LANES)], axis=0)
 
     def run_pass(p, kind):
         now = 2 if kind == "first" else p % 2
@@ -207,8 +217,7 @@
             bf[rows, :] = bbuf[now, i // 2, i % 2].astype(F32).reshape(r * 2 * heads, LANES)
             return carry
         lax.fori_loop(0, n // r, widen_bias, 0)
-        mask_row = (maskb if kind == "first" else mbuf)[...]
-        mask = jnp.concatenate([jnp.broadcast_to(mask_row[t:t + 1], (LANES, LANES)).T for t in range(n // LANES)], axis=0)
+        mask = masks[0 if kind == "first" else 1]
         for h in range(heads):
             halves = [bf[pl.ds(half * heads + h, n, stride=2 * heads), :] * LOG2E for half in range(2)]
             if kind == "first":
@@ -220,13 +229,18 @@
         base = hslot if kind == "first" else slot
         of = home_of if kind == "last" else cube_of
 
-        def post(first_row, count):
+        def post(first_row, count, bias_count):
             rows = pl.ds(first_row, count)
+            bias_rows_ = pl.ds(first_row + count - bias_count, bias_count)
             for s in range(nm):
-                u = shifted(base, s)
-                target = of(crop, u)
-                if kind != "last" and s % 2 == 0:
-                    send(bout.at[rows], bbuf.at[later, base // 2, core, rows], bs, br.at[later], target, kind, s)
+                if cube and kind == "mid":
+                    u = lows[s // sub] * sub + places[s % sub]
+                    target = lines[s // sub], stretch[s % sub]
+                else:
+                    u = shifted(base, s)
+                    target = of(crop, u)
+                if kind != "last" and s % 2 == 0 and bias_count:
+                    send(bout.at[bias_rows_], bbuf.at[later, base // 2, core, bias_rows_], bs, br.at[later], target, kind, s)
                 send(zout.at[rows, pl.ds(pl.multiple_of(u * r, r), r)],
                      zbuf.at[later, pl.ds(base * r + first_row, count)], zs, zr.at[later], target, kind, s)
 
@@ -252,11 +266,11 @@
                 send(zrelay.at[to, rows, cols], zbuf.at[later, pl.ds(me_p * r + i * count, count)],
                      zs, zr.at[later], (me_d, u), "mid", s)
 
-        def attend(first_row, count, chunk):
+        def attend(first_row, count, chunks):
             par = small[p]
             w = par[0:2]
             out_b = par[3:4]
-            gate_b = jnp.broadcast_to(par[2:3], (n, hd)).T
+            gate_b = jnp.concatenate([gt[p]] * (n // LANES), axis=1)
             zrows, keys, queries, values, gates, raw, outs, news = [], [], [], [], [], [], [], []
             units = [(q, h) for q in range(count) for h in range(heads)]
 
@@ -284,8 +298,10 @@
             def finish_row(q):
                 if kind != "last":
                     bout[first_row + q] = bias_rows(news[q].astype(F32), small[p + 1], wb[p + 1])
-                if (q + 1) % chunk == 0 and not (cube and kind == "first"):
-                    post(first_row + q + 1 - chunk, chunk)
+                if q + 1 in chunks and not (cube and kind == "first"):
+                    since = max((e for e in chunks if e <= q), default=0)
+                    whole = (q + 1) % BIAS_ROWS == 0
+                    post(first_row + since, q + 1 - since, BIAS_ROWS if whole else 0)
 
             for q in range(min(AHEAD, count)):
                 project(q)
@@ -312,10 +328,10 @@
             update(count - 1)
             finish_row(count - 1)
 
-        block, chunk = (ROWS, CHUNK) if kind == "mid" else (EDGE_ROWS, EDGE_ROWS)
+        block, chunks = (ROWS, CHUNKS) if kind == "mid" else (EDGE_ROWS, (EDGE_ROWS,))
 
         def step(i, carry):
-            attend(i * block, block, chunk)
+            attend(i * block, block, chunks)
             if cube and kind == "first":
                 spread(i, block)
                 pl.when(i > 0)(lambda: relay(i - 1, block))
@@ -381,6 +397,8 @@
                 pltpu.VMEM((heads, n, n), F32),
                 pltpu.VMEM((8, LANES), F32),
                 pltpu.VMEM((m, 3 * hd, c), BF16),
+                pltpu.VMEM((m, hd, LANES), F32),
+                pltpu.VMEM((2, n, LANES), F32),
                 pltpu.VMEM((4, r, n // 4, c), BF16),
                 pltpu.VMEM((4, r, 2 * heads, LANES), BF16),
                 pltpu.SemaphoreType.DMA,

time: 408 us -> 398 us (0.975)
  Pallas kernels: 400 us -> 386 us
    pallas_call x1, Pallas kernels: 400 us -> 386 us  [local(): pl.pallas_call(functools.partial(_kernel, nd, nm), out_shape=jax.ShapeDty...]
where the time goes in v5:
time: 398 us; the launch traced here: 394 us
  Pallas kernels  386 us (97%)
  local copies, waits for them, and re-layouts  4.28 us (1%)
    pallas_call x1, Pallas kernels, local(): pl.pallas_call(functools.partial(_kernel, nd, nm), out_shape=jax.ShapeDty...  386 us

profile of v5, /device:TPU:21, one launch (start us, length us, event | category | flops | bytes accessed | tf_op | source)
XLA Modules:
  0.0 393.8 jit_solution(4474913149496141798)
XLA Ops:
  0.0 0.7 fusion
  0.7 0.6 pad.4.maskb
  1.3 0.7 copy.9
  2.0 0.7 copy.10
  2.7 1.3 maximum_convert_fusion.small
  4.0 1.4 pad_maximum_fusion.wb
  5.4 386.1 %shard_map.82 = bf16[16,256,128]{2,1,0:T(8,128)(2,1)} custom-call(bf16[16,256,128]{2,1,0:T(8,128)(2,1)} %zin.1, f32[8,128]{1,0:T(8,128)} %pad.4.maskb, f32[16,4,128]{2,1,0:T(4,128)} %maximum_convert_fusion.small, bf16[16,128,512]{2,1,0:T(8,128)(2,1)} %bitcast.10, bf16[16,8,128]{2,1,0:T(8,128)(2,1)} %pad_maximum_fusion.wb, bf16[16,128,128]{2,1,0:T(8,128)(2,1)} %bitcast.11), custom_call_target="tpu_custom_call" | custom-call | tf_op jit(solution)/shard_map/pallas_call | solution.py:385
  391.5 2.3 copy.12
